TPU v7x, 32 devices: a whole 2x2x4 slice. The times are simulated.
32 devices in a mesh: genome: 8 (over z, x), samples: 4 (over y, core).
Axes of the slice: x: 2, y: 2, z: 4, core: 2. Of those that a mesh axis runs over, the one named last changes fastest.
Arguments:
- genotypes: int32 [4096, 12288], P('samples', 'genome'), may hold values from 0 to 2
- residuals: bfloat16 [4096, 64], P('samples'), may hold values from -78 to 78
- variant_class: int32 [12288], P('genome'), may hold values from 0 to 7
- class_weight: float32 [8], replicated, may hold values from 0.25 to 4
- gene_start: int32 [512], P(('genome', 'samples')), may hold values from 0 to 12287, as said below
- gene_end: int32 [512], P(('genome', 'samples')), may hold values from 1 to 12288, as said below
Outputs:
- score_track: float32 [12288, 64], P(('genome', 'samples'))
- gene_stat: float32 [512, 64], P(('genome', 'samples'))
Inputs may be any that keep to these rules, and one draw needn't show every extreme that they name: gene_end[g] - 1 lies in [k * 384, (k + 1) * 384) with k = g // 16. 1 <= gene_end[g] - gene_start[g] <= 384.
All inputs are finite; a program needn't handle non-finite values.
Results may differ from a plain program's by a relative error of at most 0.0003.
Values sent between devices are 32-bit elements; how exact they have to be, the bound alone decides.
No kernel may reach another device: no remote copies, remote signals or barrier semaphores. Data moves between devices by JAX's collectives and lax.ppermute only.
A program may use at most 64 MiB of HBM per device.

v0:
```python
import jax
import jax.numpy as jnp
from jax import lax
from jax.sharding import PartitionSpec as P


def prefix(x, axis, combine, identity):
    peers, place = (lax.axis_size(axis), lax.axis_index(axis))
    everything = jax.tree.map(lambda part: lax.all_gather(part, axis), x)
    start = jax.tree.map(
        lambda part, zero: jnp.broadcast_to(jnp.asarray(zero, part.dtype), part.shape), x, identity
    )

    def step(k, before):
        reached = k < place
        new = combine(before, jax.tree.map(lambda part: part[k], everything))
        return jax.tree.map(lambda a, b: jnp.where(reached, a, b), new, before)

    return lax.fori_loop(0, peers, step, start)


def passed_along(value, axis, steps):
    count = lax.axis_size(axis)
    leading, last = (max(0, -steps), min(count, count - steps))
    return lax.ppermute(value, axis, [(source, source + steps) for source in range(leading, last)])


def add_pairs(earlier, later):
    return (earlier[0] + later[0], earlier[1] + later[1])


def prefix_rows(values):
    rows, columns = values.shape
    block_width = 128
    block_count = rows // block_width
    positions = jnp.arange(block_width)
    lower_ones = (positions[:, None] >= positions[None, :]).astype(jnp.float32)
    blocks = values.reshape(block_count, block_width, columns)
    inner_sums = jnp.einsum("ij,bjk->bik", lower_ones, blocks, precision=lax.Precision.HIGHEST)
    totals = inner_sums[:, -1, :]
    before = jnp.cumsum(totals, axis=0) - totals
    return (inner_sums + before[:, None, :]).reshape(rows, columns)


def local(genotypes, residuals, variant_class, class_weight, gene_start, gene_end):
    groups = lax.axis_size("samples")
    genome_count = lax.axis_size("genome")
    sample_rows, block_vars = genotypes.shape
    phenos = residuals.shape[1]
    share_rows = block_vars // groups
    total_samples = sample_rows * groups
    total_vars = block_vars * genome_count
    sample_part = lax.axis_index("samples")
    flat_index = lax.axis_index("genome") * groups + sample_part
    contract = (((0,), (0,)), ((), ()))
    dosage = genotypes.astype(jnp.bfloat16)
    partial_value = lax.dot_general(dosage, residuals, contract, preferred_element_type=jnp.float32)
    squared = lax.dot_general(
        dosage * dosage,
        jnp.ones((sample_rows,), jnp.bfloat16),
        contract,
        preferred_element_type=jnp.float32,
    )
    spread_local = jnp.sum(jnp.square(residuals.astype(jnp.float32)), axis=0)
    carry_zero = (jnp.zeros((phenos,), jnp.float32), jnp.zeros((), jnp.float32))
    summed, counts, spread_sum = lax.psum((partial_value, squared, spread_local), "samples")
    classes = jnp.arange(class_weight.shape[0], dtype=jnp.int32)
    weight = jnp.sum(
        jnp.where(variant_class[:, None] == classes[None, :], class_weight[None, :], 0.0), axis=1
    )
    scores = summed * weight[:, None] * total_samples ** (-0.5)
    quad_terms = weight * weight * counts / total_samples
    local_prefix = prefix_rows(scores)
    local_quad = prefix_rows(quad_terms[:, None])[:, 0]
    ends = (local_prefix[-1], local_quad[-1])
    carry_sum, carry_quad = prefix(ends, "genome", add_pairs, carry_zero)
    full_prefix = local_prefix + carry_sum[None, :]
    source, quad_source = (local_prefix, local_quad)
    last_rows = source[block_vars - share_rows :]
    last_quad = quad_source[block_vars - share_rows :]
    incoming, incoming_quad = passed_along((last_rows, last_quad), "genome", 1)
    incoming = incoming - incoming[-1][None, :]
    incoming_quad = incoming_quad - incoming_quad[-1]
    near_start = jnp.maximum(sample_part - 1, 0) * share_rows
    own_start = sample_part * share_rows
    near_rows = lax.dynamic_slice_in_dim(source, near_start, share_rows, 0)
    near_quad = lax.dynamic_slice_in_dim(quad_source, near_start, share_rows, 0)
    at_first = sample_part == 0
    prior_rows = jnp.where(at_first, incoming, near_rows)
    prior_quad = jnp.where(at_first, incoming_quad, near_quad)
    own_rows = lax.dynamic_slice_in_dim(source, own_start, share_rows, 0)
    own_quad = lax.dynamic_slice_in_dim(quad_source, own_start, share_rows, 0)
    track_rows = lax.dynamic_slice_in_dim(full_prefix, own_start, share_rows, 0)
    window = jnp.concatenate([prior_rows, own_rows], axis=0)
    quad_window = jnp.concatenate([prior_quad, own_quad], axis=0)
    window_base = (flat_index - 1) * share_rows
    positions = jnp.arange(2 * share_rows, dtype=jnp.int32)
    end_pos = gene_end - 1 - window_base
    start_pos = gene_start - 1 - window_base
    picker = (positions[None, :] == end_pos[:, None]).astype(jnp.float32) - (
        positions[None, :] == start_pos[:, None]
    ).astype(jnp.float32)
    gene_score = jnp.dot(
        picker, window, precision=lax.Precision.HIGHEST, preferred_element_type=jnp.float32
    )
    gene_quad = jnp.dot(
        picker, quad_window, precision=lax.Precision.HIGHEST, preferred_element_type=jnp.float32
    )
    variance = spread_sum / total_samples + 1e-05
    gene_stat = jnp.square(gene_score) / (variance[None, :] * (gene_quad[:, None] + 1.0))
    return (track_rows * total_vars ** (-0.5), gene_stat)


def solution(mesh):
    return jax.shard_map(
        local,
        mesh=mesh,
        in_specs=(
            P("samples", "genome"),
            P("samples", None),
            P("genome"),
            P(),
            P(("genome", "samples")),
            P(("genome", "samples")),
        ),
        out_specs=(P(("genome", "samples"), None), P(("genome", "samples"), None)),
        check_vma=False,
    )
```

profile of v0, /device:TPU:8, one launch (start us, length us, event | category | flops | bytes accessed | tf_op | source)
XLA Modules:
  0.0 94.8 jit_solution(5725585461801807206)
XLA Ops:
  7.2 0.0 copy-start
  7.2 0.0 copy-start.1
  7.2 0.0 copy-start.2
  7.2 0.0 copy-start.3
  7.2 0.0 copy-start.4
  7.2 0.0 all-reduce.3.cloned.1.call-start
  7.3 3.4 %fusion.6 = f32[1536]{0:T(1024)S(1)} fusion(s32[1024,1536]{1,0:T(8,128)} %param.8), kind=kOutput, calls=%fused_computation.11 | convolution fusion | flops 6291456 | bytes 6297600 | tf_op jit(solution)/shard_map/dot_general | solution.py:58
  10.7 0.0 copy-done
  10.7 0.1 multiply_reduce_fusion
  10.8 7.2 %all-reduce = (f32[1536]{0:T(1024)S(1)}, f32[64]{0:T(128)S(1)}) all-reduce(f32[1536]{0:T(1024)S(1)} %fusion.6, f32[64]{0:T(128)S(1)} %multiply_reduce_fusion), channel_id=1, replica_groups=mesh['genome'=8,'samples'=4] {'samples'}, use_global_device_ids=true, to_apply=%region_7.8 | all-reduce | flops 1600 | bytes 12800 | tf_op jit(solution)/shard_map/psum | solution.py:66
  18.1 0.0 copy-done.1
  18.1 0.0 copy-done.2
  18.1 0.1 select_reduce_fusion
  18.2 0.1 fusion.16
  18.3 0.1 slice.41
  18.4 0.1 reduce_window_sum.23
  18.5 0.2 subtract_reduce_fusion
  18.7 0.1 broadcast_add_fusion.1
  18.8 3.4 %collective-permute-start.1 = (f32[384]{0:T(512)S(1)}, f32[384]{0:T(512)S(1)}, u32[]{:S(2)}, u32[]{:S(2)}) collective-permute-start(f32[384]{0:T(512)S(1)} %slice_bitcast_fusion.1), channel_id=1, source_target_pairs={{0,4},{4,8},{8,12},{12,16},{16,20},{20,24},{24,28},{1,5},{5,9},{9,... | collective-permute-start | bytes 4616 | tf_op jit(solution)/shard_map/ppermute | solution.py:25
  22.2 4.2 %fusion.3 = f32[1536,64]{0,1:T(8,128)} fusion(bf16[1024,64]{0,1:T(8,128)(2,1)S(1)} %copy-done, s32[1024,1536]{1,0:T(8,128)} %param.8), kind=kOutput, calls=%fused_computation.5 | convolution fusion | flops 202899456 | bytes 6815744 | tf_op jit(solution)/shard_map/dot_general | solution.py:57
  26.4 0.0 all-reduce.3.cloned.1.call-update
  26.4 0.1 fusion.35
  26.5 0.0 copy-done.3
  26.5 0.0 copy-done.4
  26.5 0.0 collective-permute-done.1
  26.5 0.6 slice.36
  27.2 0.7 dynamic-slice_select_fusion.1
  27.9 0.2 fusion.9
  28.1 30.5 %all-reduce.3.cloned.1.call-done = f32[1536,64]{0,1:T(8,128)} async-done(((f32[1536,64]{0,1:T(8,128)}), f32[1536,64]{0,1:T(8,128)}) %all-reduce.3.cloned.1.call-update) | async-done | bytes 393232 | tf_op jit(solution)/shard_map/psum | solution.py:66
  58.7 1.3 %convolution_bitcast_fusion = f32[12,128,64]{1,2,0:T(8,128)S(1)} fusion(f32[1536,64]{0,1:T(8,128)} %all-reduce.3.cloned.1.call-done, f32[1536]{0:T(1024)S(1)} %select_reduce_fusion), kind=kOutput, calls=%fused_computation.8 | convolution fusion | flops 151207936 | bytes 792576 | tf_op jit(solution)/shard_map/ij,bjk->bik/dot_general | solution.py:39
  60.0 0.4 fusion.32
  60.4 0.2 copy_bitcast_fusion
  60.6 0.2 broadcast_add_fusion
  60.8 0.2 slice_reduce_fusion.1
  60.9 17.8 %all-gather = f32[8,1,64]{2,1,0:T(1,128)S(1)} all-gather(f32[1,1,64]{2,1,0:T(1,128)S(1)} %bitcast.46), channel_id=1, replica_groups=mesh['genome'=8,'samples'=4] {'genome'}, dimensions={0}, use_global_device_ids=true | all-gather | bytes 2304 | tf_op jit(solution)/shard_map/all_gather | solution.py:9
  78.7 1.9 %collective-permute-start = (f32[384,64]{0,1:T(8,128)S(1)}, f32[384,64]{0,1:T(8,128)S(1)}, u32[]{:S(2)}, u32[]{:S(2)}) collective-permute-start(f32[384,64]{0,1:T(8,128)S(1)} %copy_bitcast_fusion.1), channel_id=1, source_target_pairs={{0,4},{4,8},{8,12},{12,16},{16,20},{20,24},{24,28},{1,5},{5,9},{9,... | collective-permute-start | bytes 294920 | tf_op jit(solution)/shard_map/ppermute | solution.py:25
  80.7 0.3 while.14
  81.0 5.2 %collective-permute-done = f32[384,64]{0,1:T(8,128)S(1)} collective-permute-done((f32[384,64]{0,1:T(8,128)S(1)}, f32[384,64]{0,1:T(8,128)S(1)}, u32[]{:S(2)}, u32[]{:S(2)}) %collective-permute-start) | collective-permute-done | bytes 98336 | tf_op jit(solution)/shard_map/ppermute | solution.py:25
  86.1 0.2 slice_reduce_fusion
  86.3 0.7 add_multiply_fusion
  87.0 0.9 fusion.5
  (15 shorter events, 0.2 us)
Async XLA Ops:
  7.2 3.5 %copy-start = (bf16[1024,64]{0,1:T(8,128)(2,1)S(1)}, bf16[1024,64]{0,1:T(8,128)(2,1)}, u32[]{:S(2)}) copy-start(bf16[1024,64]{0,1:T(8,128)(2,1)} %param.9) | copy-start | bytes 393220
  7.2 10.9 %copy-start.1 = (s32[1536]{0:T(1024)S(1)}, s32[1536]{0:T(1024)}, u32[]{:S(2)}) copy-start(s32[1536]{0:T(1024)} %param.10) | copy-start | bytes 18436
  7.2 10.9 %copy-start.2 = (f32[8]{0:T(128)S(1)}, f32[8]{0:T(128)}, u32[]{:S(2)}) copy-start(f32[8]{0:T(128)} %param.11) | copy-start | bytes 100
  7.2 19.3 %copy-start.3 = (s32[16]{0:T(128)S(1)}, s32[16]{0:T(128)}, u32[]{:S(2)}) copy-start(s32[16]{0:T(128)} %param.12) | copy-start | bytes 196
  7.2 19.3 %copy-start.4 = (s32[16]{0:T(128)S(1)}, s32[16]{0:T(128)}, u32[]{:S(2)}) copy-start(s32[16]{0:T(128)} %param.13) | copy-start | bytes 196
  7.2 51.4 %all-reduce.3.cloned.1.call-start = ((), (), s32[]{:S(2)}) async-start(), calls=%async_computation | async-start | bytes 786432 | tf_op jit(solution)/shard_map/psum | solution.py:66
  18.8 7.8 %collective-permute-start.1 = (f32[384]{0:T(512)S(1)}, f32[384]{0:T(512)S(1)}, u32[]{:S(2)}, u32[]{:S(2)}) collective-permute-start(f32[384]{0:T(512)S(1)} %slice_bitcast_fusion.1), channel_id=1, source_target_pairs={{0,4},{4,8},{8,12},{12,16},{16,20},{20,24},{24,28},{1,5},{5,9},{9,... | collective-permute-start | bytes 4616 | tf_op jit(solution)/shard_map/ppermute | solution.py:25
  78.7 7.4 %collective-permute-start = (f32[384,64]{0,1:T(8,128)S(1)}, f32[384,64]{0,1:T(8,128)S(1)}, u32[]{:S(2)}, u32[]{:S(2)}) collective-permute-start(f32[384,64]{0,1:T(8,128)S(1)} %copy_bitcast_fusion.1), channel_id=1, source_target_pairs={{0,4},{4,8},{8,12},{12,16},{16,20},{20,24},{24,28},{1,5},{5,9},{9,... | collective-permute-start | bytes 294920 | tf_op jit(solution)/shard_map/ppermute | solution.py:25
Sparse Core Ops, SparseCore 0:
  26.5 32.0 all-reduce.2
where the time goes:
time: 95.5 us; the launch traced here: 94.8 us
  waiting for transfers between devices  35.7 us (37%)
  blocking collectives  25 us (26%)
  between operations  14.2 us (15%)
  matrix products  10.2 us (11%)
  starting transfers between devices  5.36 us (6%)
  other arithmetic  2.97 us (3%)
  local copies, waits for them, and re-layouts  1.11 us (1%)
    psum x1, waiting for transfers between devices, local(): lax.psum((partial_value, squared, spread_local), 'samples')  30.5 us
    all_gather x1, blocking collectives, prefix(): everything = jax.tree.map(lambda part: lax.all_gather(part, axis), x)  17.8 us
    psum x1, blocking collectives, local(): lax.psum((partial_value, squared, spread_local), 'samples')  7.24 us
    ppermute x2, starting transfers between devices, passed_along(): lax.ppermute(value, axis, [(source, source + steps) for source in range(l...  5.32 us
    ppermute x2, waiting for transfers between devices, passed_along(): lax.ppermute(value, axis, [(source, source + steps) for source in range(l...  5.16 us
    dot_general x1, matrix products, local(): lax.dot_general(dosage, residuals, contract, preferred_element_type=jnp.f...  4.2 us
    dot_general x1, matrix products, local(): lax.dot_general(dosage * dosage, jnp.ones((sample_rows,), jnp.bfloat16),...  3.45 us
  transfers between devices with their start and end apart: 3, of which 2 were waited for; matrix products, arithmetic and copies ran while one was open for 6% of the time, Pallas kernels for 0%

commit v1 on v0

v1 whole, which is shorter than its diff:
```python
import jax
import jax.numpy as jnp
from jax import lax
from jax.experimental import pallas as pl
from jax.experimental.pallas import tpu as pltpu
from jax.sharding import PartitionSpec as P

F32, BF16 = jnp.float32, jnp.bfloat16
TN = (((0,), (0,)), ((), ()))
NT = (((1,), (1,)), ((), ()))
NN = (((1,), (0,)), ((), ()))
LANES = 128
SUBLANES = 8
VMEM_LIMIT = 16 * 2**20


def rounded(size, unit):
    return (size + unit - 1) // unit * unit


def visit_order(groups):
    masks, bit = [0], groups // 2
    while bit:
        masks = [mask | bit for mask in masks] + masks
        bit //= 2
    return masks


def split(x):
    high = x.astype(BF16)
    rest = x - high.astype(F32)
    middle = rest.astype(BF16)
    return high, middle, (rest - middle.astype(F32)).astype(BF16)


def exact_dot(a, b, dims):
    return sum(lax.dot_general(a, part, dims, preferred_element_type=F32) for part in split(b))


def exact_dot_left(a, b, dims):
    return sum(lax.dot_general(part, b, dims, preferred_element_type=F32) for part in split(a))


def first_kernel(total_samples, groups):
    def body(class_weight, genotypes, residuals, classes, send, keep, buffer, sems):
        phenos, rows = residuals.shape
        share = send.shape[2]
        me = lax.axis_index("samples")
        extra = send.shape[1] - phenos
        order = [me ^ mask for mask in visit_order(groups)]

        def copy(step):
            start = pl.multiple_of(order[step] * share, LANES)
            return pltpu.make_async_copy(
                genotypes.at[:, pl.ds(start, share)], buffer.at[step], sems.at[step]
            )

        for step in range(groups):
            copy(step).start()
        res = residuals[...]
        res32 = res.astype(F32)
        ones = jnp.ones((extra, rows), BF16)
        row_of = lax.broadcasted_iota(jnp.int32, (extra, LANES), 0)
        spread = exact_dot(ones, jnp.square(res32), NT)
        small = jnp.where(
            row_of == groups + 1,
            jnp.concatenate([spread, jnp.zeros((extra, LANES - phenos), F32)], axis=1),
            0.0,
        )
        mark_rows = lax.broadcasted_iota(jnp.int32, (extra, share), 0)
        for step in range(groups):
            copy(step).wait()
            dosage = buffer[step].astype(F32)
            part = lax.dot_general(
                res, dosage.astype(BF16), NN, preferred_element_type=F32
            )
            counts = jnp.sum(dosage * dosage, axis=0, keepdims=True)
            kind = classes[:, pl.ds(pl.multiple_of(order[step] * share, LANES), share)]
            weight = jnp.zeros((1, share), F32)
            for c in range(class_weight.shape[0]):
                weight = jnp.where(kind == c, class_weight[c], weight)
            scores = part * (weight * total_samples ** (-0.5))
            quad = weight * weight * counts / total_samples
            out = send if step < groups // 2 else keep
            slot = step % (groups // 2)
            out[slot, :phenos, :] = scores
            out[slot, phenos:, :] = jnp.where(mark_rows == 0, quad, 0.0)
            both = jnp.concatenate(
                [scores, jnp.broadcast_to(quad, (LANES - phenos, share))], axis=0
            )
            mark = (mark_rows == order[step] + 1).astype(F32).astype(BF16)
            small = small + exact_dot(mark, both, NT)
        for out in (send, keep):
            head = out[0, phenos:, :LANES]
            out[0, phenos:, :LANES] = jnp.where(row_of == 0, head, small)

    return body


def first_variant(real_share):
    groups = lax.axis_size("samples")
    return (lax.axis_index("genome") * groups + lax.axis_index("samples")) * real_share


def second_kernel(groups, real_share):
    def body(start_ref, end_ref, pair, received, fin, prefix, totals, own_genes):
        phenos = prefix.shape[0]
        share = prefix.shape[1]
        genes = own_genes.shape[0]
        me = lax.axis_index("samples")
        extra = totals.shape[0]
        block = pair[1] + received[...]
        fin[...] = block
        small = pair[0, phenos:, :LANES] + received[phenos:, :LANES]
        rows = lax.broadcasted_iota(jnp.int32, (share, share), 0)
        cols = lax.broadcasted_iota(jnp.int32, (share, share), 1)
        upper = (rows <= cols).astype(F32).astype(BF16)
        scores = block[:phenos]
        prefix[...] = exact_dot_left(scores, upper, NN)
        row_of = lax.broadcasted_iota(jnp.int32, (extra, LANES), 0)
        is_total = (row_of >= 1) & (row_of <= groups)
        whole = jnp.sum(jnp.where(is_total, small, 0.0), axis=0, keepdims=True)
        before = jnp.sum(
            jnp.where(is_total & (row_of < me + 1), small, 0.0), axis=0, keepdims=True
        )
        spread = jnp.sum(jnp.where(row_of == groups + 1, small, 0.0), axis=0, keepdims=True)
        totals[...] = jnp.where(
            row_of == 0, whole, jnp.where(row_of == 1, before, jnp.where(row_of == 2, spread, 0.0))
        )
        own_genes[...] = gene_sums(start_ref, end_ref, first_variant(real_share), block, genes)

    return body


def gene_sums(start_ref, end_ref, base, block, genes):
    share = block.shape[1]
    index = lax.broadcasted_iota(jnp.int32, (genes, 1), 0)
    start = jnp.zeros((genes, 1), jnp.int32)
    end = jnp.zeros((genes, 1), jnp.int32)
    for g in range(genes):
        start = jnp.where(index == g, start_ref[g] - base, start)
        end = jnp.where(index == g, end_ref[g] - base, end)
    spot = lax.broadcasted_iota(jnp.int32, (genes, share), 1)
    inside = ((spot >= start) & (spot < end)).astype(F32).astype(BF16)
    return exact_dot(inside, block, NT)


def third_kernel(total_samples, total_vars, real_share):
    def body(start_ref, end_ref, prefix, carry, totals, earlier, own_genes, track, stat):
        phenos, share = prefix.shape
        genes = own_genes.shape[0]
        row_of = lax.broadcasted_iota(jnp.int32, totals.shape, 0)
        rows = totals[...]
        base = jnp.where(row_of == 0, carry[0:1, :], jnp.where(row_of == 1, rows, 0.0))
        ones = jnp.where(
            lax.broadcasted_iota(jnp.int32, (rows.shape[0], share), 0) < 2, 1.0, 0.0
        ).astype(BF16)
        lifted = exact_dot_left(base, ones, TN)[:phenos]
        track[...] = (prefix[...] + lifted) * total_vars ** (-0.5)
        sums = own_genes[...] + gene_sums(
            start_ref, end_ref, first_variant(real_share) - real_share, earlier[...], genes
        )
        variance = rows[2:3, :phenos] / total_samples + 1e-05
        quad = sums[:, phenos : phenos + 1]
        stat[...] = jnp.square(sums[:, :phenos]) / (variance * (quad + 1.0))

    return body


def call(body, name, ins, outs, final=False, **more):
    spaces = {"s": pltpu.SMEM, "v": pltpu.VMEM, "h": pltpu.HBM}
    args = [
        x if kind == "s" else pltpu.with_memory_space_constraint(x, spaces[kind])
        for kind, x in ins
    ]
    result = jax.ShapeDtypeStruct if final else pltpu.VMEM
    return pl.pallas_call(
        body,
        in_specs=[pl.BlockSpec(memory_space=spaces[kind]) for kind, _ in ins],
        out_specs=[pl.BlockSpec(memory_space=pltpu.VMEM)] * len(outs),
        out_shape=[result(shape, F32) for shape in outs],
        compiler_params=pltpu.CompilerParams(vmem_limit_bytes=VMEM_LIMIT),
        name=name,
        **more,
    )(*args)


def local(genotypes, residuals, variant_class, class_weight, gene_start, gene_end):
    groups = lax.axis_size("samples")
    blocks = lax.axis_size("genome")
    both_axes = ("genome", "samples")
    sample_rows, block_vars = genotypes.shape
    phenos = residuals.shape[1]
    genes = gene_start.shape[0]
    real_share = block_vars // groups
    share = rounded(real_share, LANES)
    total_samples = sample_rows * groups
    total_vars = block_vars * blocks
    block_index = lax.axis_index("genome").astype(jnp.int32)
    extra = rounded(groups + 2, SUBLANES)
    rows = phenos + extra
    half = groups // 2
    classes = variant_class.reshape(1, block_vars)
    if share != real_share:
        missing = share - real_share
        classes = jnp.pad(variant_class.reshape(groups, real_share), ((0, 0), (0, missing)))
        classes = classes.reshape(1, groups * share)
        genotypes = jnp.pad(
            genotypes.reshape(sample_rows, groups, real_share), ((0, 0), (0, 0), (0, missing))
        ).reshape(sample_rows, groups * share)

    send, keep = call(
        first_kernel(total_samples, groups),
        "first",
        [("s", class_weight), ("h", genotypes), ("v", residuals.T), ("v", classes)],
        [(half, rows, share)] * 2,
        scratch_shapes=[
            pltpu.VMEM((groups, sample_rows, share), jnp.int32),
            pltpu.SemaphoreType.DMA((groups,)),
        ],
    )

    bit = 1
    pair = keep + lax.ppermute(send, "samples", [(i, i ^ bit) for i in range(groups)])
    while half > 2:
        bit, half = 2 * bit, half // 2
        small = jnp.pad(
            pair[:1, phenos + 1 :, :LANES], ((0, half - 1), (phenos + 1, 0), (0, share - LANES))
        )
        other = lax.ppermute(pair[:half], "samples", [(i, i ^ bit) for i in range(groups)])
        pair = pair[half:] + other + small
    bit *= 2
    received = lax.ppermute(pair[0], "samples", [(i, i ^ bit) for i in range(groups)])

    fin, prefix, totals, own_genes = call(
        second_kernel(groups, real_share),
        "second",
        [("s", gene_start), ("s", gene_end), ("v", pair), ("v", received)],
        [(rows, share), (phenos, share), (extra, LANES), (genes, rows)],
    )

    last = groups * blocks
    even = lax.ppermute(fin, both_axes, [(k, k + 1) for k in range(0, last, 2)])
    odd = lax.ppermute(fin, both_axes, [(k, k + 1) for k in range(1, last - 1, 2)])
    whole = totals[:1]
    carry = jnp.zeros_like(whole)
    bit = 1
    while bit < blocks:
        one_way = 2 * bit >= blocks
        pairs = [(k, k ^ bit) for k in range(blocks) if not (one_way and k & bit)]
        other = lax.ppermute(whole, "genome", pairs)
        carry = carry + jnp.where((block_index & bit) != 0, other, 0.0)
        whole = whole + other
        bit *= 2

    track, stat = call(
        third_kernel(total_samples, total_vars, real_share),
        "third",
        [("s", gene_start), ("s", gene_end)]
        + [("v", x) for x in (prefix, carry, totals, even + odd, own_genes)],
        [(phenos, share), (genes, phenos)],
        final=True,
    )
    return track[:, :real_share].T, stat


def solution(mesh):
    return jax.shard_map(
        local,
        mesh=mesh,
        in_specs=(
            P("samples", "genome"),
            P("samples", None),
            P("genome"),
            P(),
            P(("genome", "samples")),
            P(("genome", "samples")),
        ),
        out_specs=(P(("genome", "samples"), None), P(("genome", "samples"), None)),
        check_vma=False,
    )
```

time: 95.5 us -> 37.6 us (0.39)
  blocking collectives: 25 us -> 0 us
  waiting for transfers between devices: 35.7 us -> 17 us
  between operations: 14.2 us -> 0.74 us
  matrix products: 10.2 us -> 0 us
  Pallas kernels: 0 us -> 6.69 us
  starting transfers between devices: 5.36 us -> 10.5 us
  other arithmetic: 2.97 us -> 0.06 us
  local copies, waits for them, and re-layouts: 1.11 us -> 2.29 us
    psum x1 -> x0, waiting for transfers between devices: 30.5 us -> none  [local(): lax.psum((partial_value, squared, spread_local), 'samples')]
    all_gather x1 -> x0, blocking collectives: 17.8 us -> none  [prefix(): everything = jax.tree.map(lambda part: lax.all_gather(part, axis), x)]
    ppermute x2 -> x7, waiting for transfers between devices: 5.16 us -> 17 us  [the longest x1 6.53 us: local(): lax.ppermute(fin, both_axes, [(k, k + 1) for k in range(1, last - 1, 2)])]
    dot_general x6 -> x0, matrix products: 10.2 us -> none  [the longest x1 4.2 us: local(): lax.dot_general(dosage, residuals, contract, preferred_element_type=jnp.f...]
    psum x1 -> x0, blocking collectives: 7.24 us -> none  [local(): lax.psum((partial_value, squared, spread_local), 'samples')]
    pallas_call x0 -> x3, Pallas kernels: none -> 6.69 us  [call(): pl.pallas_call(body, in_specs=[pl.BlockSpec(memory_space=spaces[kind]) fo...]
    ppermute x2 -> x7, starting transfers between devices: 5.32 us -> 10.5 us  [the longest x3 6.27 us: local(): other = lax.ppermute(whole, 'genome', pairs)]
    unnamed x10 -> x8, local copies, waits for them, and re-layouts: 0.02 us -> 1.57 us
  transfers between devices with their start and end apart: 3 -> 7, of which waited for: 2 -> 5; matrix products, arithmetic and copies ran while one was open for 6% -> 0% of each run, Pallas kernels for 0% -> 0%
where the time goes in v1:
time: 37.6 us; the launch traced here: 37.3 us
  waiting for transfers between devices  17 us (45%)
  starting transfers between devices  10.5 us (28%)
  Pallas kernels  6.69 us (18%)
  local copies, waits for them, and re-layouts  2.29 us (6%)
  between operations  0.74 us (2%)
    pallas_call x3, Pallas kernels, call(): pl.pallas_call(body, in_specs=[pl.BlockSpec(memory_space=spaces[kind]) fo...  6.69 us
    ppermute x1, waiting for transfers between devices, local(): lax.ppermute(fin, both_axes, [(k, k + 1) for k in range(1, last - 1, 2)])  6.53 us
    ppermute x3, starting transfers between devices, local(): other = lax.ppermute(whole, 'genome', pairs)  6.27 us
    ppermute x3, waiting for transfers between devices, local(): other = lax.ppermute(whole, 'genome', pairs)  5.42 us
    ppermute x1, waiting for transfers between devices, local(): lax.ppermute(pair[0], 'samples', [(i, i ^ bit) for i in range(groups)])  3.58 us
    ppermute x1, starting transfers between devices, local(): lax.ppermute(pair[0], 'samples', [(i, i ^ bit) for i in range(groups)])  1.58 us
    unnamed x8, local copies, waits for them, and re-layouts  1.57 us
    ppermute x1, waiting for transfers between devices, local(): lax.ppermute(send, 'samples', [(i, i ^ bit) for i in range(groups)])  1.46 us
  transfers between devices with their start and end apart: 7, of which 5 were waited for; matrix products, arithmetic and copies ran while one was open for 0% of the time, Pallas kernels for 0%

profile of v1, /device:TPU:8, one launch (start us, length us, event | category | flops | bytes accessed | tf_op | source)
XLA Modules:
  0.0 37.3 jit_solution(17160320542226819647)
XLA Ops:
  0.6 0.0 copy-start.1
  0.6 0.0 copy-start.2
  0.7 0.7 %reshape.7.classes = s32[1,1536]{1,0:T(1,128)S(1)} reshape(s32[1536]{0:T(1024)} %param.8) | data formatting | bytes 12288 | tf_op jit(solution)/shard_map/reshape | solution.py:203
  1.4 0.0 copy-start
  1.4 0.9 %copy-done = bf16[1024,64]{0,1:T(8,128)(2,1)S(1)} copy-done((bf16[1024,64]{0,1:T(8,128)(2,1)S(1)}, bf16[1024,64]{0,1:T(8,128)(2,1)}, u32[]{:S(2)}) %copy-start) | copy-done | bytes 131096
  2.3 0.0 copy-start.3
  2.3 0.7 %copy-done.3 = f32[8]{0:T(128)S(1)} copy-done((f32[8]{0:T(128)S(1)}, f32[8]{0:T(128)}, u32[]{:S(2)}) %copy-start.3) | copy-done | bytes 56
  2.9 4.3 %first.1 = (f32[2,72,384]{2,1,0:T(8,128)S(1)}, f32[2,72,384]{2,1,0:T(8,128)S(1)}) custom-call(f32[8]{0:T(128)S(1)} %copy-done.3, s32[1024,1536]{1,0:T(8,128)} %genotypes.1, bf16[64,1024]{1,0:T(8,128)(2,1)S(1)} %bitcast.4, s32[1,1536]{1,0:T(1,128)S(1)} %reshape.7.classes), custom_call_target="tpu_custom_call" | custom-call | tf_op jit(solution)/shard_map/first/pallas_call | solution.py:177
  7.2 0.1 collective-permute-start
  7.3 1.5 %collective-permute-done = f32[2,72,384]{2,1,0:T(8,128)S(1)} collective-permute-done((f32[2,72,384]{2,1,0:T(8,128)S(1)}, f32[2,72,384]{2,1,0:T(8,128)S(1)}, u32[]{:S(2)}, u32[]{:S(2)}) %collective-permute-start) | collective-permute-done | bytes 221216 | tf_op jit(solution)/shard_map/ppermute | solution.py:224
  8.8 1.6 %collective-permute-start.1 = (f32[72,384]{1,0:T(8,128)S(1)}, f32[72,384]{1,0:T(8,128)S(1)}, u32[]{:S(2)}, u32[]{:S(2)}) collective-permute-start(f32[72,384]{1,0:T(8,128)S(1)} %slice_bitcast_fusion), channel_id=1, source_target_pairs={{0,2},{1,3},{2,0},{3,1},{4,6},{5,7},{6,4},{7,5},{8,10},{9,11},{10,... | collective-permute-start | bytes 331784 | tf_op jit(solution)/shard_map/ppermute | solution.py:233
  10.4 3.6 %collective-permute-done.1.received = f32[72,384]{1,0:T(8,128)S(1)} collective-permute-done((f32[72,384]{1,0:T(8,128)S(1)}, f32[72,384]{1,0:T(8,128)S(1)}, u32[]{:S(2)}, u32[]{:S(2)}) %collective-permute-start.1) | collective-permute-done | bytes 110624 | tf_op jit(solution)/shard_map/ppermute | solution.py:233
  14.0 0.0 copy-done.1
  14.0 0.0 copy-done.2
  14.0 0.8 %second.1 = (f32[72,384]{1,0:T(8,128)S(1)}, f32[64,384]{1,0:T(8,128)S(1)}, f32[8,128]{1,0:T(8,128)S(1)}, f32[16,72]{1,0:T(8,128)S(1)}) custom-call(s32[16]{0:T(128)S(1)} %copy-done.1, s32[16]{0:T(128)S(1)} %copy-done.2, f32[2,72,384]{2,1,0:T(8,128)S(1)} %add.18.pair, f32[72,384]{1,0:T(8,128)S(1)} %collective-permute-done.1.received), custom_call_target="tpu_custom_call" | custom-call | tf_op jit(solution)/shard_map/second/pallas_call | solution.py:177
  14.8 1.6 %collective-permute-start.2 = (f32[1,128]{1,0:T(1,128)S(1)}, f32[1,128]{1,0:T(1,128)S(1)}, u32[]{:S(2)}, u32[]{:S(2)}) collective-permute-start(f32[1,128]{1,0:T(1,128)S(1)} %slice.7), channel_id=1, source_target_pairs={{0,4},{4,0},{8,12},{12,8},{16,20},{20,16},{24,28},{28,24},{1,5},{5... | collective-permute-start | bytes 1544 | tf_op jit(solution)/shard_map/ppermute | solution.py:251
  16.4 2.1 %collective-permute-done.2 = f32[1,128]{1,0:T(1,128)S(1)} collective-permute-done((f32[1,128]{1,0:T(1,128)S(1)}, f32[1,128]{1,0:T(1,128)S(1)}, u32[]{:S(2)}, u32[]{:S(2)}) %collective-permute-start.2) | collective-permute-done | bytes 544 | tf_op jit(solution)/shard_map/ppermute | solution.py:251
  18.5 0.2 collective-permute-start.3
  18.7 3.3 %collective-permute-done.3 = f32[1,128]{1,0:T(1,128)S(1)} collective-permute-done((f32[1,128]{1,0:T(1,128)S(1)}, f32[1,128]{1,0:T(1,128)S(1)}, u32[]{:S(2)}, u32[]{:S(2)}) %collective-permute-start.3) | collective-permute-done | bytes 544 | tf_op jit(solution)/shard_map/ppermute | solution.py:251
  22.1 4.5 %collective-permute-start.4 = (f32[1,128]{1,0:T(1,128)S(1)}, f32[1,128]{1,0:T(1,128)S(1)}, u32[]{:S(2)}, u32[]{:S(2)}) collective-permute-start(f32[1,128]{1,0:T(1,128)S(1)} %add.21), channel_id=1, source_target_pairs={{0,16},{4,20},{8,24},{12,28},{1,17},{5,21},{9,25},{13,29},{2,18},{... | collective-permute-start | bytes 1544 | tf_op jit(solution)/shard_map/ppermute | solution.py:251
  26.6 1.3 %collective-permute-start.5 = (f32[72,384]{1,0:T(8,128)S(1)}, f32[72,384]{1,0:T(8,128)S(1)}, u32[]{:S(2)}, u32[]{:S(2)}) collective-permute-start(f32[72,384]{1,0:T(8,128)S(1)} %get-tuple-element.14), channel_id=1, source_target_pairs={{0,1},{2,3},{4,5},{6,7},{8,9},{10,11},{12,13},{14,15},{16,17},{18,... | collective-permute-start | bytes 331784 | tf_op jit(solution)/shard_map/ppermute | solution.py:243
  27.9 1.3 %collective-permute-start.6 = (f32[72,384]{1,0:T(8,128)S(1)}, f32[72,384]{1,0:T(8,128)S(1)}, u32[]{:S(2)}, u32[]{:S(2)}) collective-permute-start(f32[72,384]{1,0:T(8,128)S(1)} %get-tuple-element.14), channel_id=1, source_target_pairs={{1,2},{3,4},{5,6},{7,8},{9,10},{11,12},{13,14},{15,16},{17,18},{19... | collective-permute-start | bytes 331784 | tf_op jit(solution)/shard_map/ppermute | solution.py:244
  29.2 0.0 collective-permute-done.4
  29.2 0.0 collective-permute-done.5
  29.2 6.5 %collective-permute-done.6 = f32[72,384]{1,0:T(8,128)S(1)} collective-permute-done((f32[72,384]{1,0:T(8,128)S(1)}, f32[72,384]{1,0:T(8,128)S(1)}, u32[]{:S(2)}, u32[]{:S(2)}) %collective-permute-start.6) | collective-permute-done | bytes 110624 | tf_op jit(solution)/shard_map/ppermute | solution.py:244
  35.7 1.5 %third.1 = (f32[64,384]{1,0:T(8,128)}, f32[16,64]{1,0:T(8,128)}) custom-call(s32[16]{0:T(128)S(1)} %copy-done.1, s32[16]{0:T(128)S(1)} %copy-done.2, f32[64,384]{1,0:T(8,128)S(1)} %get-tuple-element.12.prefix, f32[1,128]{1,0:T(1,128)S(1)} %fusion.1.carry, f32[8,128]{1,0:T(8,128)S(1)} %get-tuple-element.13.totals, f32[72,384]{1,0:T(8,128)S(1)} %add.23.earlier, ...), custom_call_target="tpu_custom_call" | custom-call | tf_op jit(solution)/shard_map/third/pallas_call | solution.py:177
  (7 shorter events, 0.1 us)
Async XLA Ops:
  0.6 13.4 %copy-start.1 = (s32[16]{0:T(128)S(1)}, s32[16]{0:T(128)}, u32[]{:S(2)}) copy-start(s32[16]{0:T(128)} %start_ref.3) | copy-start | bytes 196
  0.6 13.4 %copy-start.2 = (s32[16]{0:T(128)S(1)}, s32[16]{0:T(128)}, u32[]{:S(2)}) copy-start(s32[16]{0:T(128)} %end_ref.3) | copy-start | bytes 196
  1.4 0.9 %copy-start = (bf16[1024,64]{0,1:T(8,128)(2,1)S(1)}, bf16[1024,64]{0,1:T(8,128)(2,1)}, u32[]{:S(2)}) copy-start(bf16[1024,64]{0,1:T(8,128)(2,1)} %param.7) | copy-start | bytes 393220
  2.3 0.7 %copy-start.3 = (f32[8]{0:T(128)S(1)}, f32[8]{0:T(128)}, u32[]{:S(2)}) copy-start(f32[8]{0:T(128)} %class_weight.1) | copy-start | bytes 100
  7.2 1.5 %collective-permute-start = (f32[2,72,384]{2,1,0:T(8,128)S(1)}, f32[2,72,384]{2,1,0:T(8,128)S(1)}, u32[]{:S(2)}, u32[]{:S(2)}) collective-permute-start(f32[2,72,384]{2,1,0:T(8,128)S(1)} %get-tuple-element.11), channel_id=1, source_target_pairs={{0,1},{1,0},{2,3},{3,2},{4,5},{5,4},{6,7},{7,6},{8,9},{9,8},{10,11... | collective-permute-start | bytes 663560 | tf_op jit(solution)/shard_map/ppermute | solution.py:224
  8.8 5.2 %collective-permute-start.1 = (f32[72,384]{1,0:T(8,128)S(1)}, f32[72,384]{1,0:T(8,128)S(1)}, u32[]{:S(2)}, u32[]{:S(2)}) collective-permute-start(f32[72,384]{1,0:T(8,128)S(1)} %slice_bitcast_fusion), channel_id=1, source_target_pairs={{0,2},{1,3},{2,0},{3,1},{4,6},{5,7},{6,4},{7,5},{8,10},{9,11},{10,... | collective-permute-start | bytes 331784 | tf_op jit(solution)/shard_map/ppermute | solution.py:233
  14.8 3.6 %collective-permute-start.2 = (f32[1,128]{1,0:T(1,128)S(1)}, f32[1,128]{1,0:T(1,128)S(1)}, u32[]{:S(2)}, u32[]{:S(2)}) collective-permute-start(f32[1,128]{1,0:T(1,128)S(1)} %slice.7), channel_id=1, source_target_pairs={{0,4},{4,0},{8,12},{12,8},{16,20},{20,16},{24,28},{28,24},{1,5},{5... | collective-permute-start | bytes 1544 | tf_op jit(solution)/shard_map/ppermute | solution.py:251
  18.5 3.6 %collective-permute-start.3 = (f32[1,128]{1,0:T(1,128)S(1)}, f32[1,128]{1,0:T(1,128)S(1)}, u32[]{:S(2)}, u32[]{:S(2)}) collective-permute-start(f32[1,128]{1,0:T(1,128)S(1)} %slice_add_fusion), channel_id=1, source_target_pairs={{0,8},{4,12},{8,0},{12,4},{16,24},{20,28},{24,16},{28,20},{1,9},{5... | collective-permute-start | bytes 1544 | tf_op jit(solution)/shard_map/ppermute | solution.py:251
  22.1 7.1 %collective-permute-start.4 = (f32[1,128]{1,0:T(1,128)S(1)}, f32[1,128]{1,0:T(1,128)S(1)}, u32[]{:S(2)}, u32[]{:S(2)}) collective-permute-start(f32[1,128]{1,0:T(1,128)S(1)} %add.21), channel_id=1, source_target_pairs={{0,16},{4,20},{8,24},{12,28},{1,17},{5,21},{9,25},{13,29},{2,18},{... | collective-permute-start | bytes 1544 | tf_op jit(solution)/shard_map/ppermute | solution.py:251
  26.6 2.6 %collective-permute-start.5 = (f32[72,384]{1,0:T(8,128)S(1)}, f32[72,384]{1,0:T(8,128)S(1)}, u32[]{:S(2)}, u32[]{:S(2)}) collective-permute-start(f32[72,384]{1,0:T(8,128)S(1)} %get-tuple-element.14), channel_id=1, source_target_pairs={{0,1},{2,3},{4,5},{6,7},{8,9},{10,11},{12,13},{14,15},{16,17},{18,... | collective-permute-start | bytes 331784 | tf_op jit(solution)/shard_map/ppermute | solution.py:243
  27.9 7.9 %collective-permute-start.6 = (f32[72,384]{1,0:T(8,128)S(1)}, f32[72,384]{1,0:T(8,128)S(1)}, u32[]{:S(2)}, u32[]{:S(2)}) collective-permute-start(f32[72,384]{1,0:T(8,128)S(1)} %get-tuple-element.14), channel_id=1, source_target_pairs={{1,2},{3,4},{5,6},{7,8},{9,10},{11,12},{13,14},{15,16},{17,18},{19... | collective-permute-start | bytes 331784 | tf_op jit(solution)/shard_map/ppermute | solution.py:244

commit v2 on v1

--- a/solution.py
+++ b/solution.py
@@ -42,7 +42,10 @@
 
 
 def first_kernel(total_samples, groups):
-    def body(class_weight, genotypes, residuals, classes, send, keep, buffer, sems):
+    def body(
+        weight_hbm, genotypes, residuals_hbm, classes_hbm, send, keep,
+        buffer, sems, class_weight, residuals, classes, small_sems,
+    ):
         phenos, rows = residuals.shape
         share = send.shape[2]
         me = lax.axis_index("samples")
@@ -55,8 +58,18 @@
                 genotypes.at[:, pl.ds(start, share)], buffer.at[step], sems.at[step]
             )
 
+        small_copies = [
+            pltpu.make_async_copy(source, target, small_sems.at[k])
+            for k, (source, target) in enumerate(
+                [(residuals_hbm, residuals), (classes_hbm, classes), (weight_hbm, class_weight)]
+            )
+        ]
+        for each in small_copies:
+            each.start()
         for step in range(groups):
             copy(step).start()
+        for each in small_copies:
+            each.wait()
         res = residuals[...]
         res32 = res.astype(F32)
         ones = jnp.ones((extra, rows), BF16)
@@ -75,7 +88,7 @@
                 res, dosage.astype(BF16), NN, preferred_element_type=F32
             )
             counts = jnp.sum(dosage * dosage, axis=0, keepdims=True)
-            kind = classes[:, pl.ds(pl.multiple_of(order[step] * share, LANES), share)]
+            kind = classes[pl.ds(pl.multiple_of(order[step] * share, LANES), share)].reshape(1, share)
             weight = jnp.zeros((1, share), F32)
             for c in range(class_weight.shape[0]):
                 weight = jnp.where(kind == c, class_weight[c], weight)
@@ -146,7 +159,7 @@
 
 
 def third_kernel(total_samples, total_vars, real_share):
-    def body(start_ref, end_ref, prefix, carry, totals, earlier, own_genes, track, stat):
+    def body(start_ref, end_ref, prefix, carry, totals, near, far, own_genes, track, stat):
         phenos, share = prefix.shape
         genes = own_genes.shape[0]
         row_of = lax.broadcasted_iota(jnp.int32, totals.shape, 0)
@@ -157,8 +170,10 @@
         ).astype(BF16)
         lifted = exact_dot_left(base, ones, TN)[:phenos]
         track[...] = (prefix[...] + lifted) * total_vars ** (-0.5)
+        odd = lax.axis_index("samples") % 2 == 1
+        earlier = jnp.where(odd, near[...], far[...])
         sums = own_genes[...] + gene_sums(
-            start_ref, end_ref, first_variant(real_share) - real_share, earlier[...], genes
+            start_ref, end_ref, first_variant(real_share) - real_share, earlier, genes
         )
         variance = rows[2:3, :phenos] / total_samples + 1e-05
         quad = sums[:, phenos : phenos + 1]
@@ -185,6 +200,28 @@
     )(*args)
 
 
+def block_prefix(whole, blocks, groups):
+    devices = blocks * groups
+    index = lax.axis_index("genome")
+    both_axes = ("genome", "samples")
+
+    def exchange(x, mask):
+        return lax.ppermute(x, both_axes, [(k, k ^ mask ^ 1) for k in range(devices)])
+
+    carry = jnp.zeros_like(whole)
+    bit = 1
+    while bit < blocks:
+        other = exchange(whole, bit * groups)
+        carry = carry + jnp.where((index & bit) != 0, other, 0.0)
+        whole = whole + other
+        bit *= 2
+    bit = 2
+    while bit < groups:
+        carry = carry + exchange(carry, bit)
+        bit *= 2
+    return carry
+
+
 def local(genotypes, residuals, variant_class, class_weight, gene_start, gene_end):
     groups = lax.axis_size("samples")
     blocks = lax.axis_size("genome")
@@ -196,15 +233,15 @@
     share = rounded(real_share, LANES)
     total_samples = sample_rows * groups
     total_vars = block_vars * blocks
-    block_index = lax.axis_index("genome").astype(jnp.int32)
     extra = rounded(groups + 2, SUBLANES)
     rows = phenos + extra
+    devices = groups * blocks
     half = groups // 2
-    classes = variant_class.reshape(1, block_vars)
+    classes = variant_class
     if share != real_share:
         missing = share - real_share
         classes = jnp.pad(variant_class.reshape(groups, real_share), ((0, 0), (0, missing)))
-        classes = classes.reshape(1, groups * share)
+        classes = classes.reshape(groups * share)
         genotypes = jnp.pad(
             genotypes.reshape(sample_rows, groups, real_share), ((0, 0), (0, 0), (0, missing))
         ).reshape(sample_rows, groups * share)
@@ -212,11 +249,15 @@
     send, keep = call(
         first_kernel(total_samples, groups),
         "first",
-        [("s", class_weight), ("h", genotypes), ("v", residuals.T), ("v", classes)],
+        [("h", class_weight), ("h", genotypes), ("h", residuals.T), ("h", classes)],
         [(half, rows, share)] * 2,
         scratch_shapes=[
             pltpu.VMEM((groups, sample_rows, share), jnp.int32),
             pltpu.SemaphoreType.DMA((groups,)),
+            pltpu.SMEM(class_weight.shape, F32),
+            pltpu.VMEM((phenos, sample_rows), BF16),
+            pltpu.VMEM((groups * share,), jnp.int32),
+            pltpu.SemaphoreType.DMA((3,)),
         ],
     )
 
@@ -229,6 +270,8 @@
         )
         other = lax.ppermute(pair[:half], "samples", [(i, i ^ bit) for i in range(groups)])
         pair = pair[half:] + other + small
+    whole = jnp.sum(pair[0, phenos + 1 : phenos + 1 + groups, :LANES], axis=0, keepdims=True)
+    carry = block_prefix(whole, blocks, groups)
     bit *= 2
     received = lax.ppermute(pair[0], "samples", [(i, i ^ bit) for i in range(groups)])
 
@@ -239,25 +282,14 @@
         [(rows, share), (phenos, share), (extra, LANES), (genes, rows)],
     )
 
-    last = groups * blocks
-    even = lax.ppermute(fin, both_axes, [(k, k + 1) for k in range(0, last, 2)])
-    odd = lax.ppermute(fin, both_axes, [(k, k + 1) for k in range(1, last - 1, 2)])
-    whole = totals[:1]
-    carry = jnp.zeros_like(whole)
-    bit = 1
-    while bit < blocks:
-        one_way = 2 * bit >= blocks
-        pairs = [(k, k ^ bit) for k in range(blocks) if not (one_way and k & bit)]
-        other = lax.ppermute(whole, "genome", pairs)
-        carry = carry + jnp.where((block_index & bit) != 0, other, 0.0)
-        whole = whole + other
-        bit *= 2
+    near = lax.ppermute(fin, both_axes, [(k, k ^ 1) for k in range(devices)])
+    far = lax.ppermute(fin, both_axes, [(k, k + 1) for k in range(1, devices - 1, 2)])
 
     track, stat = call(
         third_kernel(total_samples, total_vars, real_share),
         "third",
         [("s", gene_start), ("s", gene_end)]
-        + [("v", x) for x in (prefix, carry, totals, even + odd, own_genes)],
+        + [("v", x) for x in (prefix, carry, totals, near, far, own_genes)],
         [(phenos, share), (genes, phenos)],
         final=True,
     )

time: 37.6 us -> 25.9 us (0.69)
  waiting for transfers between devices: 17 us -> 7.8 us
  local copies, waits for them, and re-layouts: 2.29 us -> 0.02 us
    ppermute x5 -> x6, waiting for transfers between devices: 11.9 us -> 6.34 us  [the longest x4 4.45 us: exchange(): lax.ppermute(x, both_axes, [(k, k ^ mask ^ 1) for k in range(devices)])]
    ppermute x1, waiting for transfers between devices: 3.58 us -> 0.01 us  [local(): lax.ppermute(pair[0], 'samples', [(i, i ^ bit) for i in range(groups)])]
    unnamed x8 -> x4, local copies, waits for them, and re-layouts: 1.57 us -> 0.01 us
    reshape x1 -> x0, local copies, waits for them, and re-layouts: 0.71 us -> none  [local(): classes = variant_class.reshape(1, block_vars)]
    ppermute x5 -> x6, starting transfers between devices: 8.86 us -> 8.7 us  [the longest x4 7.28 us: exchange(): lax.ppermute(x, both_axes, [(k, k ^ mask ^ 1) for k in range(devices)])]
  transfers between devices with their start and end apart: 7 -> 8, of which waited for: 5 -> 5; matrix products, arithmetic and copies ran while one was open for 0% -> 0% of each run, Pallas kernels for 0% -> 3%
where the time goes in v2:
time: 25.9 us; the launch traced here: 25.7 us
  starting transfers between devices  10.4 us (40%)
  waiting for transfers between devices  7.8 us (30%)
  Pallas kernels  6.78 us (26%)
  between operations  0.71 us (3%)
    ppermute x4, starting transfers between devices, exchange(): lax.ppermute(x, both_axes, [(k, k ^ mask ^ 1) for k in range(devices)])  7.28 us
    pallas_call x3, Pallas kernels, call(): pl.pallas_call(body, in_specs=[pl.BlockSpec(memory_space=spaces[kind]) fo...  6.78 us
    ppermute x4, waiting for transfers between devices, exchange(): lax.ppermute(x, both_axes, [(k, k ^ mask ^ 1) for k in range(devices)])  4.45 us
    ppermute x1, waiting for transfers between devices, local(): lax.ppermute(fin, both_axes, [(k, k + 1) for k in range(1, devices - 1, 2)])  1.88 us
    ppermute x1, starting transfers between devices, local(): lax.ppermute(pair[0], 'samples', [(i, i ^ bit) for i in range(groups)])  1.58 us
    ppermute x1, waiting for transfers between devices, local(): lax.ppermute(send, 'samples', [(i, i ^ bit) for i in range(groups)])  1.46 us
    ppermute x1, starting transfers between devices, local(): lax.ppermute(fin, both_axes, [(k, k + 1) for k in range(1, devices - 1, 2)])  1.28 us
  transfers between devices with their start and end apart: 8, of which 5 were waited for; matrix products, arithmetic and copies ran while one was open for 0% of the time, Pallas kernels for 3%

profile of v2, /device:TPU:8, one launch (start us, length us, event | category | flops | bytes accessed | tf_op | source)
XLA Modules:
  0.0 25.7 jit_solution(12061373440653665155)
XLA Ops:
  0.6 0.0 copy-start
  0.6 0.0 copy-start.1
  0.7 4.4 %first.1 = (f32[2,72,384]{2,1,0:T(8,128)S(1)}, f32[2,72,384]{2,1,0:T(8,128)S(1)}) custom-call(f32[8]{0:T(128)} %weight_hbm.1, s32[1024,1536]{1,0:T(8,128)} %genotypes.1, bf16[64,1024]{1,0:T(8,128)(2,1)} %bitcast.6, s32[1536]{0:T(1024)} %classes_hbm.1), custom_call_target="tpu_custom_call" | custom-call | tf_op jit(solution)/shard_map/first/pallas_call | solution.py:192
  5.0 0.1 collective-permute-start
  5.1 1.5 %collective-permute-done = f32[2,72,384]{2,1,0:T(8,128)S(1)} collective-permute-done((f32[2,72,384]{2,1,0:T(8,128)S(1)}, f32[2,72,384]{2,1,0:T(8,128)S(1)}, u32[]{:S(2)}, u32[]{:S(2)}) %collective-permute-start) | collective-permute-done | bytes 221216 | tf_op jit(solution)/shard_map/ppermute | solution.py:265
  6.6 1.3 %collective-permute-start.2 = (f32[1,128]{1,0:T(1,128)S(1)}, f32[1,128]{1,0:T(1,128)S(1)}, u32[]{:S(2)}, u32[]{:S(2)}) collective-permute-start(f32[1,128]{1,0:T(1,128)S(1)} %bitcast.7), channel_id=1, source_target_pairs={{0,5},{1,4},{2,7},{3,6},{4,1},{5,0},{6,3},{7,2},{8,13},{9,12},{10,... | collective-permute-start | bytes 1544 | tf_op jit(solution)/shard_map/ppermute | solution.py:209
  7.9 1.6 %collective-permute-start.1 = (f32[72,384]{1,0:T(8,128)S(1)}, f32[72,384]{1,0:T(8,128)S(1)}, u32[]{:S(2)}, u32[]{:S(2)}) collective-permute-start(f32[72,384]{1,0:T(8,128)S(1)} %slice_bitcast_fusion), channel_id=1, source_target_pairs={{0,2},{1,3},{2,0},{3,1},{4,6},{5,7},{6,4},{7,5},{8,10},{9,11},{10,... | collective-permute-start | bytes 331784 | tf_op jit(solution)/shard_map/ppermute | solution.py:276
  9.5 0.2 collective-permute-done.2
  9.7 0.0 collective-permute-start.3
  9.7 3.0 %collective-permute-done.3 = f32[1,128]{1,0:T(1,128)S(1)} collective-permute-done((f32[1,128]{1,0:T(1,128)S(1)}, f32[1,128]{1,0:T(1,128)S(1)}, u32[]{:S(2)}, u32[]{:S(2)}) %collective-permute-start.3) | collective-permute-done | bytes 544 | tf_op jit(solution)/shard_map/ppermute | solution.py:209
  12.7 2.6 %collective-permute-start.4 = (f32[1,128]{1,0:T(1,128)S(1)}, f32[1,128]{1,0:T(1,128)S(1)}, u32[]{:S(2)}, u32[]{:S(2)}) collective-permute-start(f32[1,128]{1,0:T(1,128)S(1)} %add.21), channel_id=1, source_target_pairs={{0,17},{1,16},{2,19},{3,18},{4,21},{5,20},{6,23},{7,22},{8,25},{9,... | collective-permute-start | bytes 1544 | tf_op jit(solution)/shard_map/ppermute | solution.py:209
  15.3 0.0 collective-permute-done.1.received
  15.3 0.0 copy-done
  15.3 0.0 copy-done.1
  15.3 0.9 %second.1 = (f32[72,384]{1,0:T(8,128)S(1)}, f32[64,384]{1,0:T(8,128)S(1)}, f32[8,128]{1,0:T(8,128)S(1)}, f32[16,72]{1,0:T(8,128)S(1)}) custom-call(s32[16]{0:T(128)S(1)} %copy-done, s32[16]{0:T(128)S(1)} %copy-done.1, f32[2,72,384]{2,1,0:T(8,128)S(1)} %add.18.pair, f32[72,384]{1,0:T(8,128)S(1)} %collective-permute-done.1.received), custom_call_target="tpu_custom_call" | custom-call | tf_op jit(solution)/shard_map/second/pallas_call | solution.py:192
  16.2 0.1 collective-permute-start.6
  16.3 1.3 %collective-permute-start.7 = (f32[72,384]{1,0:T(8,128)S(1)}, f32[72,384]{1,0:T(8,128)S(1)}, u32[]{:S(2)}, u32[]{:S(2)}) collective-permute-start(f32[72,384]{1,0:T(8,128)S(1)} %get-tuple-element.14), channel_id=1, source_target_pairs={{1,2},{3,4},{5,6},{7,8},{9,10},{11,12},{13,14},{15,16},{17,18},{19... | collective-permute-start | bytes 331784 | tf_op jit(solution)/shard_map/ppermute | solution.py:286
  17.6 0.0 collective-permute-done.4
  17.6 3.4 %collective-permute-start.5 = (f32[1,128]{1,0:T(1,128)S(1)}, f32[1,128]{1,0:T(1,128)S(1)}, u32[]{:S(2)}, u32[]{:S(2)}) collective-permute-start(f32[1,128]{1,0:T(1,128)S(1)} %fusion.1), channel_id=1, source_target_pairs={{0,3},{1,2},{2,1},{3,0},{4,7},{5,6},{6,5},{7,4},{8,11},{9,10},{10,... | collective-permute-start | bytes 1544 | tf_op jit(solution)/shard_map/ppermute | solution.py:209
  21.0 1.3 %collective-permute-done.5 = f32[1,128]{1,0:T(1,128)S(1)} collective-permute-done((f32[1,128]{1,0:T(1,128)S(1)}, f32[1,128]{1,0:T(1,128)S(1)}, u32[]{:S(2)}, u32[]{:S(2)}) %collective-permute-start.5) | collective-permute-done | bytes 544 | tf_op jit(solution)/shard_map/ppermute | solution.py:209
  22.3 0.0 collective-permute-done.6.near
  22.3 1.9 %collective-permute-done.7.far = f32[72,384]{1,0:T(8,128)S(1)} collective-permute-done((f32[72,384]{1,0:T(8,128)S(1)}, f32[72,384]{1,0:T(8,128)S(1)}, u32[]{:S(2)}, u32[]{:S(2)}) %collective-permute-start.7) | collective-permute-done | bytes 110624 | tf_op jit(solution)/shard_map/ppermute | solution.py:286
  24.2 1.5 %third.1 = (f32[64,384]{1,0:T(8,128)}, f32[16,64]{1,0:T(8,128)}) custom-call(s32[16]{0:T(128)S(1)} %copy-done, s32[16]{0:T(128)S(1)} %copy-done.1, f32[64,384]{1,0:T(8,128)S(1)} %get-tuple-element.12.prefix, f32[1,128]{1,0:T(1,128)S(1)} %add.23.carry, f32[8,128]{1,0:T(8,128)S(1)} %get-tuple-element.13.totals, f32[72,384]{1,0:T(8,128)S(1)} %collective-permute-done.6.near, ...), custom_call_target="tpu_custom_call" | custom-call | tf_op jit(solution)/shard_map/third/pallas_call | solution.py:192
  (7 shorter events, 0.1 us)
Async XLA Ops:
  0.6 14.7 %copy-start = (s32[16]{0:T(128)S(1)}, s32[16]{0:T(128)}, u32[]{:S(2)}) copy-start(s32[16]{0:T(128)} %start_ref.3) | copy-start | bytes 196
  0.6 14.7 %copy-start.1 = (s32[16]{0:T(128)S(1)}, s32[16]{0:T(128)}, u32[]{:S(2)}) copy-start(s32[16]{0:T(128)} %end_ref.3) | copy-start | bytes 196
  5.0 1.5 %collective-permute-start = (f32[2,72,384]{2,1,0:T(8,128)S(1)}, f32[2,72,384]{2,1,0:T(8,128)S(1)}, u32[]{:S(2)}, u32[]{:S(2)}) collective-permute-start(f32[2,72,384]{2,1,0:T(8,128)S(1)} %get-tuple-element.11), channel_id=1, source_target_pairs={{0,1},{1,0},{2,3},{3,2},{4,5},{5,4},{6,7},{7,6},{8,9},{9,8},{10,11... | collective-permute-start | bytes 663560 | tf_op jit(solution)/shard_map/ppermute | solution.py:265
  6.6 3.1 %collective-permute-start.2 = (f32[1,128]{1,0:T(1,128)S(1)}, f32[1,128]{1,0:T(1,128)S(1)}, u32[]{:S(2)}, u32[]{:S(2)}) collective-permute-start(f32[1,128]{1,0:T(1,128)S(1)} %bitcast.7), channel_id=1, source_target_pairs={{0,5},{1,4},{2,7},{3,6},{4,1},{5,0},{6,3},{7,2},{8,13},{9,12},{10,... | collective-permute-start | bytes 1544 | tf_op jit(solution)/shard_map/ppermute | solution.py:209
  7.9 7.4 %collective-permute-start.1 = (f32[72,384]{1,0:T(8,128)S(1)}, f32[72,384]{1,0:T(8,128)S(1)}, u32[]{:S(2)}, u32[]{:S(2)}) collective-permute-start(f32[72,384]{1,0:T(8,128)S(1)} %slice_bitcast_fusion), channel_id=1, source_target_pairs={{0,2},{1,3},{2,0},{3,1},{4,6},{5,7},{6,4},{7,5},{8,10},{9,11},{10,... | collective-permute-start | bytes 331784 | tf_op jit(solution)/shard_map/ppermute | solution.py:276
  9.7 3.0 %collective-permute-start.3 = (f32[1,128]{1,0:T(1,128)S(1)}, f32[1,128]{1,0:T(1,128)S(1)}, u32[]{:S(2)}, u32[]{:S(2)}) collective-permute-start(f32[1,128]{1,0:T(1,128)S(1)} %bitcast_add_fusion), channel_id=1, source_target_pairs={{0,9},{1,8},{2,11},{3,10},{4,13},{5,12},{6,15},{7,14},{8,1},{9,0},... | collective-permute-start | bytes 1544 | tf_op jit(solution)/shard_map/ppermute | solution.py:209
  12.7 4.9 %collective-permute-start.4 = (f32[1,128]{1,0:T(1,128)S(1)}, f32[1,128]{1,0:T(1,128)S(1)}, u32[]{:S(2)}, u32[]{:S(2)}) collective-permute-start(f32[1,128]{1,0:T(1,128)S(1)} %add.21), channel_id=1, source_target_pairs={{0,17},{1,16},{2,19},{3,18},{4,21},{5,20},{6,23},{7,22},{8,25},{9,... | collective-permute-start | bytes 1544 | tf_op jit(solution)/shard_map/ppermute | solution.py:209
  16.2 6.1 %collective-permute-start.6 = (f32[72,384]{1,0:T(8,128)S(1)}, f32[72,384]{1,0:T(8,128)S(1)}, u32[]{:S(2)}, u32[]{:S(2)}) collective-permute-start(f32[72,384]{1,0:T(8,128)S(1)} %get-tuple-element.14), channel_id=1, source_target_pairs={{0,1},{1,0},{2,3},{3,2},{4,5},{5,4},{6,7},{7,6},{8,9},{9,8},{10,11... | collective-permute-start | bytes 331784 | tf_op jit(solution)/shard_map/ppermute | solution.py:285
  16.3 7.9 %collective-permute-start.7 = (f32[72,384]{1,0:T(8,128)S(1)}, f32[72,384]{1,0:T(8,128)S(1)}, u32[]{:S(2)}, u32[]{:S(2)}) collective-permute-start(f32[72,384]{1,0:T(8,128)S(1)} %get-tuple-element.14), channel_id=1, source_target_pairs={{1,2},{3,4},{5,6},{7,8},{9,10},{11,12},{13,14},{15,16},{17,18},{19... | collective-permute-start | bytes 331784 | tf_op jit(solution)/shard_map/ppermute | solution.py:286
  17.6 4.7 %collective-permute-start.5 = (f32[1,128]{1,0:T(1,128)S(1)}, f32[1,128]{1,0:T(1,128)S(1)}, u32[]{:S(2)}, u32[]{:S(2)}) collective-permute-start(f32[1,128]{1,0:T(1,128)S(1)} %fusion.1), channel_id=1, source_target_pairs={{0,3},{1,2},{2,1},{3,0},{4,7},{5,6},{6,5},{7,4},{8,11},{9,10},{10,... | collective-permute-start | bytes 1544 | tf_op jit(solution)/shard_map/ppermute | solution.py:209

commit v3 on v2

v3 whole, which is shorter than its diff:
```python
import jax
import jax.numpy as jnp
from jax import lax
from jax.experimental import pallas as pl
from jax.experimental.pallas import tpu as pltpu
from jax.sharding import PartitionSpec as P


F32, BF16 = jnp.float32, jnp.bfloat16
NT = (((1,), (1,)), ((), ()))
NN = (((1,), (0,)), ((), ()))
LANES = 128
SUBLANES = 8
VMEM_LIMIT = 16 * 2**20


def rounded(size, unit):
    return (size + unit - 1) // unit * unit


def visit_order(groups):
    masks, bit = [0], groups // 2
    while bit:
        masks = [mask | bit for mask in masks] + masks
        bit //= 2
    return masks


def split(x):
    high = x.astype(BF16)
    rest = x - high.astype(F32)
    middle = rest.astype(BF16)
    return high, middle, (rest - middle.astype(F32)).astype(BF16)


def exact_dot(a, b, dims):
    return sum(lax.dot_general(a, part, dims, preferred_element_type=F32) for part in split(b))


def exact_dot_left(a, b, dims):
    return sum(lax.dot_general(part, b, dims, preferred_element_type=F32) for part in split(a))


def first_kernel(total_samples, groups):
    def body(
        weight_hbm, genotypes, residuals_hbm, classes_hbm, send, keep,
        buffer, sums, sems, class_weight, residuals, classes, small_sems,
    ):
        phenos, rows = residuals.shape
        share = send.shape[2]
        columns = groups * share
        me = lax.axis_index("samples")
        extra = send.shape[1] - phenos
        steps = sems.shape[0]
        piece = rows // steps
        small_copies = [
            pltpu.make_async_copy(source, target, small_sems.at[k])
            for k, (source, target) in enumerate(
                [(residuals_hbm, residuals), (classes_hbm, classes), (weight_hbm, class_weight)]
            )
        ]
        copies = [
            pltpu.make_async_copy(
                genotypes.at[pl.ds(k * piece, piece), :],
                buffer.at[pl.ds(k * piece, piece), :],
                sems.at[k],
            )
            for k in range(steps)
        ]
        for each in small_copies + copies:
            each.start()
        for each in small_copies:
            each.wait()
        squares = jnp.square(residuals[...].astype(F32))
        spread = exact_dot(jnp.ones((extra, rows), BF16), squares, NT)
        kind = classes[...].reshape(1, columns)
        weight = jnp.zeros((1, columns), F32)
        for c in range(class_weight.shape[0]):
            weight = jnp.where(kind == c, class_weight[c], weight)
        for k in range(steps):
            copies[k].wait()
            spot = pl.ds(k * piece, piece)
            dosage = buffer[spot, :].astype(F32)
            part = lax.dot_general(
                residuals[:, spot], dosage.astype(BF16), NN, preferred_element_type=F32
            )
            counts = jnp.sum((dosage * dosage).reshape(-1, SUBLANES, columns), axis=0)
            if k:
                part, counts = part + sums[:phenos], counts + sums[phenos:]
            if k < steps - 1:
                sums[:phenos], sums[phenos:] = part, counts
        scores = part * (weight * total_samples ** (-0.5))
        quad = (weight * weight / total_samples) * jnp.sum(counts, axis=0, keepdims=True)
        both = jnp.concatenate([scores, jnp.broadcast_to(quad, (extra, columns))], axis=0)
        folded = []
        for c in range(groups):
            lanes = [
                both[:, c * share + b : c * share + b + LANES] for b in range(0, share, LANES)
            ]
            folded.append(sum(lanes[1:], lanes[0]))
        folded = jnp.concatenate(folded, axis=1)
        shape = (extra, groups * LANES)
        mark = lax.broadcasted_iota(jnp.int32, shape, 1) // LANES + 1
        mark = (mark == lax.broadcasted_iota(jnp.int32, shape, 0)).astype(F32).astype(BF16)
        totals = exact_dot(mark, folded, NT)
        row_of = lax.broadcasted_iota(jnp.int32, (extra, LANES), 0)
        small = jnp.concatenate([totals, jnp.zeros((extra, LANES - phenos - extra), F32)], axis=1)
        spread = jnp.concatenate([spread, jnp.zeros((extra, LANES - phenos), F32)], axis=1)
        small = jnp.where(row_of == groups + 1, spread, small)
        below = jnp.where(lax.broadcasted_iota(jnp.int32, (extra, columns), 0) == 0, quad, 0.0)
        for c in range(groups):
            for out, slot, is_here in places(send, keep, me ^ c, groups):

                @pl.when(is_here)
                def _():
                    part_of = slice(c * share, (c + 1) * share)
                    out[slot, :phenos, :] = scores[:, part_of]
                    out[slot, phenos:, :] = below[:, part_of]

        for out in (send, keep):
            out[0, phenos:, :LANES] += small

    return body


def places(send, keep, mask, groups):
    order = visit_order(groups)
    half = groups // 2
    slot = sum(
        jnp.where(mask == order[k], k % half, 0) for k in range(groups)
    )
    return [(send, slot, mask % 2 == 1), (keep, slot, mask % 2 == 0)]


def first_variant(real_share):
    groups = lax.axis_size("samples")
    return (lax.axis_index("genome") * groups + lax.axis_index("samples")) * real_share


def second_kernel(real_share):
    def body(start_ref, end_ref, block, totals, prefix, own_genes, mask):
        phenos, share = prefix.shape
        genes = own_genes.shape[0]
        me = lax.axis_index("samples")
        rows = lax.broadcasted_iota(jnp.int32, (share, share), 0)
        cols = lax.broadcasted_iota(jnp.int32, (share, share), 1)
        upper = (rows <= cols).astype(F32).astype(BF16)
        small = totals[...]
        row_of = lax.broadcasted_iota(jnp.int32, small.shape, 0)
        earlier = jnp.sum(
            jnp.where((row_of >= 1) & (row_of < me + 1), small, 0.0), axis=0, keepdims=True
        )
        inner = exact_dot_left(block[:phenos], upper, NN)
        prefix[...] = inner + column(earlier, phenos)
        base = first_variant(real_share)
        inside = window_mask(start_ref, end_ref, base, genes, share)
        own_genes[...] = exact_dot(inside.astype(BF16), block[...], NT)
        mask[...] = window_mask(start_ref, end_ref, base - real_share, genes, share)

    return body


def column(row, size):
    return jnp.transpose(jnp.broadcast_to(row, (SUBLANES, LANES)))[:size, :1]


def window_mask(start_ref, end_ref, base, genes, share):
    index = lax.broadcasted_iota(jnp.int32, (genes, 1), 0)
    start = jnp.zeros((genes, 1), jnp.int32)
    end = jnp.zeros((genes, 1), jnp.int32)
    for g in range(genes):
        start = jnp.where(index == g, start_ref[g] - base, start)
        end = jnp.where(index == g, end_ref[g] - base, end)
    spot = lax.broadcasted_iota(jnp.int32, (genes, share), 1)
    return ((spot >= start) & (spot < end)).astype(F32)


def last_kernel(total_samples, total_vars, groups):
    def body(prefix, carry, totals, near, far, own_genes, mask, track, stat):
        phenos = prefix.shape[0]
        track[...] = (prefix[...] + column(carry[...], phenos)) * total_vars ** (-0.5)
        odd = lax.axis_index("samples") % 2 == 1
        earlier = jnp.where(odd, near[...], far[...])
        sums = own_genes[...] + exact_dot(mask[...].astype(BF16), earlier, NT)
        variance = totals[groups + 1 : groups + 2, :phenos] / total_samples + 1e-05
        quad = sums[:, phenos : phenos + 1]
        stat[...] = jnp.square(sums[:, :phenos]) / (variance * (quad + 1.0))

    return body


def call(body, ins, outs, final=False, **more):
    spaces = {"s": pltpu.SMEM, "v": pltpu.VMEM, "h": pltpu.HBM}
    args = [
        x if kind == "s" else pltpu.with_memory_space_constraint(x, spaces[kind])
        for kind, x in ins
    ]
    result = jax.ShapeDtypeStruct if final else pltpu.VMEM
    return pl.pallas_call(
        body,
        in_specs=[pl.BlockSpec(memory_space=spaces[kind]) for kind, _ in ins],
        out_specs=[pl.BlockSpec(memory_space=pltpu.VMEM)] * len(outs),
        out_shape=[result(shape, F32) for shape in outs],
        compiler_params=pltpu.CompilerParams(vmem_limit_bytes=VMEM_LIMIT),
        **more,
    )(*args)


def block_prefix(whole, blocks, groups):
    devices = blocks * groups
    index = lax.axis_index("genome")
    both_axes = ("genome", "samples")

    def exchange(x, mask):
        return lax.ppermute(x, both_axes, [(k, k ^ mask ^ 1) for k in range(devices)])

    carry = jnp.zeros_like(whole)
    bit = 1
    while bit < blocks:
        other = exchange(whole, bit * groups)
        carry = carry + jnp.where((index & bit) != 0, other, 0.0)
        whole = whole + other
        bit *= 2
    bit = 2
    while bit < groups:
        carry = carry + exchange(carry, bit)
        bit *= 2
    return carry


def local(genotypes, residuals, variant_class, class_weight, gene_start, gene_end):
    groups = lax.axis_size("samples")
    blocks = lax.axis_size("genome")
    both_axes = ("genome", "samples")
    sample_rows, block_vars = genotypes.shape
    phenos = residuals.shape[1]
    genes = gene_start.shape[0]
    real_share = block_vars // groups
    share = rounded(real_share, LANES)
    total_samples = sample_rows * groups
    total_vars = block_vars * blocks
    extra = rounded(groups + 2, SUBLANES)
    rows = phenos + extra
    devices = groups * blocks
    half = groups // 2
    classes = variant_class
    if share != real_share:
        missing = share - real_share
        classes = jnp.pad(variant_class.reshape(groups, real_share), ((0, 0), (0, missing)))
        classes = classes.reshape(groups * share)
        genotypes = jnp.pad(
            genotypes.reshape(sample_rows, groups, real_share), ((0, 0), (0, 0), (0, missing))
        ).reshape(sample_rows, groups * share)

    send, keep = call(
        first_kernel(total_samples, groups),
        [("h", class_weight), ("h", genotypes), ("h", residuals.T), ("h", classes)],
        [(half, rows, share)] * 2,
        scratch_shapes=[
            pltpu.VMEM((sample_rows, groups * share), jnp.int32),
            pltpu.VMEM((phenos + SUBLANES, groups * share), F32),
            pltpu.SemaphoreType.DMA((4,)),
            pltpu.SMEM(class_weight.shape, F32),
            pltpu.VMEM((phenos, sample_rows), BF16),
            pltpu.VMEM((groups * share,), jnp.int32),
            pltpu.SemaphoreType.DMA((3,)),
        ],
    )

    bit = 1
    pair = keep + lax.ppermute(send, "samples", [(i, i ^ bit) for i in range(groups)])
    while half > 2:
        bit, half = 2 * bit, half // 2
        small = jnp.pad(
            pair[:1, phenos + 1 :, :LANES], ((0, half - 1), (phenos + 1, 0), (0, share - LANES))
        )
        other = lax.ppermute(pair[:half], "samples", [(i, i ^ bit) for i in range(groups)])
        pair = pair[half:] + other + small
    mine = pair[0, phenos:, :LANES]
    whole = jnp.sum(mine[1 : groups + 1], axis=0, keepdims=True)
    carry = block_prefix(whole, blocks, groups)
    bit *= 2
    received = lax.ppermute(pair[0], "samples", [(i, i ^ bit) for i in range(groups)])

    block = pair[1] + received
    totals = mine + received[phenos:, :LANES]
    near = lax.ppermute(block, both_axes, [(k, k ^ 1) for k in range(devices)])
    far = lax.ppermute(block, both_axes, [(k, k + 1) for k in range(1, devices - 1, 2)])
    prefix, own_genes, mask = call(
        second_kernel(real_share),
        [("s", gene_start), ("s", gene_end), ("v", block), ("v", totals)],
        [(phenos, share), (genes, rows), (genes, share)],
    )
    track, stat = call(
        last_kernel(total_samples, total_vars, groups),
        [("v", x) for x in (prefix, carry, totals, near, far, own_genes, mask)],
        [(phenos, share), (genes, phenos)],
        final=True,
    )
    return track[:, :real_share].T, stat


def solution(mesh):
    return jax.shard_map(
        local,
        mesh=mesh,
        in_specs=(
            P("samples", "genome"),
            P("samples", None),
            P("genome"),
            P(),
            P(("genome", "samples")),
            P(("genome", "samples")),
        ),
        out_specs=(P(("genome", "samples"), None), P(("genome", "samples"), None)),
        check_vma=False,
    )
```

time: 25.9 us -> 28.8 us (1.11)
  waiting for transfers between devices: 7.8 us -> 14.5 us
  starting transfers between devices: 10.4 us -> 7.97 us
  Pallas kernels: 6.78 us -> 5.38 us
    ppermute x2, waiting for transfers between devices: 1.88 us -> 5.67 us  [the longest x1 5.66 us: local(): lax.ppermute(block, both_axes, [(k, k + 1) for k in range(1, devices - 1,...]
    ppermute x4, starting transfers between devices: 7.28 us -> 4.85 us  [exchange(): lax.ppermute(x, both_axes, [(k, k ^ mask ^ 1) for k in range(devices)])]
    ppermute x4, waiting for transfers between devices: 4.45 us -> 6.75 us  [exchange(): lax.ppermute(x, both_axes, [(k, k ^ mask ^ 1) for k in range(devices)])]
    pallas_call x3, Pallas kernels: 6.78 us -> 5.38 us  [call(): pl.pallas_call(body, in_specs=[pl.BlockSpec(memory_space=spaces[kind]) fo...]
    ppermute x1, waiting for transfers between devices: 0.01 us -> 0.59 us  [local(): lax.ppermute(pair[0], 'samples', [(i, i ^ bit) for i in range(groups)])]
  transfers between devices with their start and end apart: 8 -> 8, of which waited for: 5 -> 6; matrix products, arithmetic and copies ran while one was open for 0% -> 0% of each run, Pallas kernels for 3% -> 3%
where the time goes in v3:
time: 28.8 us; the launch traced here: 28.6 us
  waiting for transfers between devices  14.5 us (50%)
  starting transfers between devices  7.97 us (28%)
  Pallas kernels  5.38 us (19%)
  between operations  0.72 us (2%)
    ppermute x4, waiting for transfers between devices, exchange(): lax.ppermute(x, both_axes, [(k, k ^ mask ^ 1) for k in range(devices)])  6.75 us
    ppermute x1, waiting for transfers between devices, local(): lax.ppermute(block, both_axes, [(k, k + 1) for k in range(1, devices - 1,...  5.66 us
    pallas_call x3, Pallas kernels, call(): pl.pallas_call(body, in_specs=[pl.BlockSpec(memory_space=spaces[kind]) fo...  5.38 us
    ppermute x4, starting transfers between devices, exchange(): lax.ppermute(x, both_axes, [(k, k ^ mask ^ 1) for k in range(devices)])  4.85 us
    ppermute x1, starting transfers between devices, local(): lax.ppermute(pair[0], 'samples', [(i, i ^ bit) for i in range(groups)])  1.58 us
    ppermute x1, waiting for transfers between devices, local(): lax.ppermute(send, 'samples', [(i, i ^ bit) for i in range(groups)])  1.46 us
    ppermute x1, starting transfers between devices, local(): lax.ppermute(block, both_axes, [(k, k + 1) for k in range(1, devices - 1,...  1.28 us
    ppermute x1, waiting for transfers between devices, local(): lax.ppermute(pair[0], 'samples', [(i, i ^ bit) for i in range(groups)])  0.59 us
  transfers between devices with their start and end apart: 8, of which 6 were waited for; matrix products, arithmetic and copies ran while one was open for 0% of the time, Pallas kernels for 3%

profile of v3, /device:TPU:8, one launch (start us, length us, event | category | flops | bytes accessed | tf_op | source)
XLA Modules:
  0.0 28.6 jit_solution(6675601703679635755)
XLA Ops:
  0.6 0.0 copy-start
  0.6 0.0 copy-start.1
  0.7 3.6 %shard_map.77 = (f32[2,72,384]{2,1,0:T(8,128)S(1)}, f32[2,72,384]{2,1,0:T(8,128)S(1)}) custom-call(f32[8]{0:T(128)} %weight_hbm.1, s32[1024,1536]{1,0:T(8,128)} %genotypes.1, bf16[64,1024]{1,0:T(8,128)(2,1)} %bitcast.14, s32[1536]{0:T(1024)} %classes_hbm.1), custom_call_target="tpu_custom_call" | custom-call | tf_op jit(solution)/shard_map/pallas_call | solution.py:199
  4.3 0.1 collective-permute-start
  4.3 1.5 %collective-permute-done = f32[2,72,384]{2,1,0:T(8,128)S(1)} collective-permute-done((f32[2,72,384]{2,1,0:T(8,128)S(1)}, f32[2,72,384]{2,1,0:T(8,128)S(1)}, u32[]{:S(2)}, u32[]{:S(2)}) %collective-permute-start) | collective-permute-done | bytes 221216 | tf_op jit(solution)/shard_map/ppermute | solution.py:271
  5.8 1.3 %collective-permute-start.2 = (f32[1,128]{1,0:T(1,128)S(1)}, f32[1,128]{1,0:T(1,128)S(1)}, u32[]{:S(2)}, u32[]{:S(2)}) collective-permute-start(f32[1,128]{1,0:T(1,128)S(1)} %bitcast.15), channel_id=1, source_target_pairs={{0,5},{1,4},{2,7},{3,6},{4,1},{5,0},{6,3},{7,2},{8,13},{9,12},{10,... | collective-permute-start | bytes 1544 | tf_op jit(solution)/shard_map/ppermute | solution.py:215
  7.1 1.8 %collective-permute-done.2 = f32[1,128]{1,0:T(1,128)S(1)} collective-permute-done((f32[1,128]{1,0:T(1,128)S(1)}, f32[1,128]{1,0:T(1,128)S(1)}, u32[]{:S(2)}, u32[]{:S(2)}) %collective-permute-start.2) | collective-permute-done | bytes 544 | tf_op jit(solution)/shard_map/ppermute | solution.py:215
  8.9 0.0 collective-permute-start.3
  8.9 3.0 %collective-permute-done.3 = f32[1,128]{1,0:T(1,128)S(1)} collective-permute-done((f32[1,128]{1,0:T(1,128)S(1)}, f32[1,128]{1,0:T(1,128)S(1)}, u32[]{:S(2)}, u32[]{:S(2)}) %collective-permute-start.3) | collective-permute-done | bytes 544 | tf_op jit(solution)/shard_map/ppermute | solution.py:215
  11.9 2.3 %collective-permute-start.4 = (f32[1,128]{1,0:T(1,128)S(1)}, f32[1,128]{1,0:T(1,128)S(1)}, u32[]{:S(2)}, u32[]{:S(2)}) collective-permute-start(f32[1,128]{1,0:T(1,128)S(1)} %add.29), channel_id=1, source_target_pairs={{0,17},{1,16},{2,19},{3,18},{4,21},{5,20},{6,23},{7,22},{8,25},{9,... | collective-permute-start | bytes 1544 | tf_op jit(solution)/shard_map/ppermute | solution.py:215
  14.2 1.6 %collective-permute-start.1 = (f32[72,384]{1,0:T(8,128)S(1)}, f32[72,384]{1,0:T(8,128)S(1)}, u32[]{:S(2)}, u32[]{:S(2)}) collective-permute-start(f32[72,384]{1,0:T(8,128)S(1)} %slice_bitcast_fusion), channel_id=1, source_target_pairs={{0,2},{1,3},{2,0},{3,1},{4,6},{5,7},{6,4},{7,5},{8,10},{9,11},{10,... | collective-permute-start | bytes 331784 | tf_op jit(solution)/shard_map/ppermute | solution.py:283
  15.8 0.0 collective-permute-done.4
  15.8 1.2 %collective-permute-start.5 = (f32[1,128]{1,0:T(1,128)S(1)}, f32[1,128]{1,0:T(1,128)S(1)}, u32[]{:S(2)}, u32[]{:S(2)}) collective-permute-start(f32[1,128]{1,0:T(1,128)S(1)} %fusion.2), channel_id=1, source_target_pairs={{0,3},{1,2},{2,1},{3,0},{4,7},{5,6},{6,5},{7,4},{8,11},{9,10},{10,... | collective-permute-start | bytes 1544 | tf_op jit(solution)/shard_map/ppermute | solution.py:215
  17.1 2.0 %collective-permute-done.5 = f32[1,128]{1,0:T(1,128)S(1)} collective-permute-done((f32[1,128]{1,0:T(1,128)S(1)}, f32[1,128]{1,0:T(1,128)S(1)}, u32[]{:S(2)}, u32[]{:S(2)}) %collective-permute-start.5) | collective-permute-done | bytes 544 | tf_op jit(solution)/shard_map/ppermute | solution.py:215
  19.1 0.6 %collective-permute-done.1 = f32[72,384]{1,0:T(8,128)S(1)} collective-permute-done((f32[72,384]{1,0:T(8,128)S(1)}, f32[72,384]{1,0:T(8,128)S(1)}, u32[]{:S(2)}, u32[]{:S(2)}) %collective-permute-start.1) | collective-permute-done | bytes 110624 | tf_op jit(solution)/shard_map/ppermute | solution.py:283
  19.7 0.2 collective-permute-start.6
  19.9 1.3 %collective-permute-start.7 = (f32[72,384]{1,0:T(8,128)S(1)}, f32[72,384]{1,0:T(8,128)S(1)}, u32[]{:S(2)}, u32[]{:S(2)}) collective-permute-start(f32[72,384]{1,0:T(8,128)S(1)} %fusion.block), channel_id=1, source_target_pairs={{1,2},{3,4},{5,6},{7,8},{9,10},{11,12},{13,14},{15,16},{17,18},{19... | collective-permute-start | bytes 331784 | tf_op jit(solution)/shard_map/ppermute | solution.py:288
  21.2 0.0 copy-done
  21.2 0.0 copy-done.1
  21.2 0.9 %shard_map.78 = (f32[64,384]{1,0:T(8,128)S(1)}, f32[16,72]{1,0:T(8,128)S(1)}, f32[16,384]{1,0:T(8,128)S(1)}) custom-call(s32[16]{0:T(128)S(1)} %copy-done, s32[16]{0:T(128)S(1)} %copy-done.1, f32[72,384]{1,0:T(8,128)S(1)} %fusion.block, f32[8,128]{1,0:T(8,128)S(1)} %slice_add_fusion.totals), custom_call_target="tpu_custom_call" | custom-call | tf_op jit(solution)/shard_map/pallas_call | solution.py:199
  22.0 0.0 collective-permute-done.6.near
  22.0 5.7 %collective-permute-done.7.far = f32[72,384]{1,0:T(8,128)S(1)} collective-permute-done((f32[72,384]{1,0:T(8,128)S(1)}, f32[72,384]{1,0:T(8,128)S(1)}, u32[]{:S(2)}, u32[]{:S(2)}) %collective-permute-start.7) | collective-permute-done | bytes 110624 | tf_op jit(solution)/shard_map/ppermute | solution.py:288
  27.7 0.9 %shard_map.79 = (f32[64,384]{1,0:T(8,128)}, f32[16,64]{1,0:T(8,128)}) custom-call(f32[64,384]{1,0:T(8,128)S(1)} %get-tuple-element.11.prefix, f32[1,128]{1,0:T(1,128)S(1)} %add.31.carry, f32[8,128]{1,0:T(8,128)S(1)} %slice_add_fusion.totals, f32[72,384]{1,0:T(8,128)S(1)} %collective-permute-done.6.near, f32[72,384]{1,0:T(8,128)S(1)} %collective-permute-done.7.far, ...), custom_call_target="tpu_custom_call" | custom-call | tf_op jit(solution)/shard_map/pallas_call | solution.py:199
  (9 shorter events, 0.1 us)
Async XLA Ops:
  0.6 20.5 %copy-start = (s32[16]{0:T(128)S(1)}, s32[16]{0:T(128)}, u32[]{:S(2)}) copy-start(s32[16]{0:T(128)} %start_ref.1) | copy-start | bytes 196
  0.6 20.5 %copy-start.1 = (s32[16]{0:T(128)S(1)}, s32[16]{0:T(128)}, u32[]{:S(2)}) copy-start(s32[16]{0:T(128)} %end_ref.1) | copy-start | bytes 196
  4.3 1.5 %collective-permute-start = (f32[2,72,384]{2,1,0:T(8,128)S(1)}, f32[2,72,384]{2,1,0:T(8,128)S(1)}, u32[]{:S(2)}, u32[]{:S(2)}) collective-permute-start(f32[2,72,384]{2,1,0:T(8,128)S(1)} %get-tuple-element.10), channel_id=1, source_target_pairs={{0,1},{1,0},{2,3},{3,2},{4,5},{5,4},{6,7},{7,6},{8,9},{9,8},{10,11... | collective-permute-start | bytes 663560 | tf_op jit(solution)/shard_map/ppermute | solution.py:271
  5.8 3.1 %collective-permute-start.2 = (f32[1,128]{1,0:T(1,128)S(1)}, f32[1,128]{1,0:T(1,128)S(1)}, u32[]{:S(2)}, u32[]{:S(2)}) collective-permute-start(f32[1,128]{1,0:T(1,128)S(1)} %bitcast.15), channel_id=1, source_target_pairs={{0,5},{1,4},{2,7},{3,6},{4,1},{5,0},{6,3},{7,2},{8,13},{9,12},{10,... | collective-permute-start | bytes 1544 | tf_op jit(solution)/shard_map/ppermute | solution.py:215
  8.9 3.0 %collective-permute-start.3 = (f32[1,128]{1,0:T(1,128)S(1)}, f32[1,128]{1,0:T(1,128)S(1)}, u32[]{:S(2)}, u32[]{:S(2)}) collective-permute-start(f32[1,128]{1,0:T(1,128)S(1)} %bitcast_add_fusion), channel_id=1, source_target_pairs={{0,9},{1,8},{2,11},{3,10},{4,13},{5,12},{6,15},{7,14},{8,1},{9,0},... | collective-permute-start | bytes 1544 | tf_op jit(solution)/shard_map/ppermute | solution.py:215
  11.9 3.9 %collective-permute-start.4 = (f32[1,128]{1,0:T(1,128)S(1)}, f32[1,128]{1,0:T(1,128)S(1)}, u32[]{:S(2)}, u32[]{:S(2)}) collective-permute-start(f32[1,128]{1,0:T(1,128)S(1)} %add.29), channel_id=1, source_target_pairs={{0,17},{1,16},{2,19},{3,18},{4,21},{5,20},{6,23},{7,22},{8,25},{9,... | collective-permute-start | bytes 1544 | tf_op jit(solution)/shard_map/ppermute | solution.py:215
  14.2 5.4 %collective-permute-start.1 = (f32[72,384]{1,0:T(8,128)S(1)}, f32[72,384]{1,0:T(8,128)S(1)}, u32[]{:S(2)}, u32[]{:S(2)}) collective-permute-start(f32[72,384]{1,0:T(8,128)S(1)} %slice_bitcast_fusion), channel_id=1, source_target_pairs={{0,2},{1,3},{2,0},{3,1},{4,6},{5,7},{6,4},{7,5},{8,10},{9,11},{10,... | collective-permute-start | bytes 331784 | tf_op jit(solution)/shard_map/ppermute | solution.py:283
  15.8 3.2 %collective-permute-start.5 = (f32[1,128]{1,0:T(1,128)S(1)}, f32[1,128]{1,0:T(1,128)S(1)}, u32[]{:S(2)}, u32[]{:S(2)}) collective-permute-start(f32[1,128]{1,0:T(1,128)S(1)} %fusion.2), channel_id=1, source_target_pairs={{0,3},{1,2},{2,1},{3,0},{4,7},{5,6},{6,5},{7,4},{8,11},{9,10},{10,... | collective-permute-start | bytes 1544 | tf_op jit(solution)/shard_map/ppermute | solution.py:215
  19.7 2.4 %collective-permute-start.6 = (f32[72,384]{1,0:T(8,128)S(1)}, f32[72,384]{1,0:T(8,128)S(1)}, u32[]{:S(2)}, u32[]{:S(2)}) collective-permute-start(f32[72,384]{1,0:T(8,128)S(1)} %fusion.block), channel_id=1, source_target_pairs={{0,1},{1,0},{2,3},{3,2},{4,5},{5,4},{6,7},{7,6},{8,9},{9,8},{10,11... | collective-permute-start | bytes 331784 | tf_op jit(solution)/shard_map/ppermute | solution.py:287
  19.9 7.9 %collective-permute-start.7 = (f32[72,384]{1,0:T(8,128)S(1)}, f32[72,384]{1,0:T(8,128)S(1)}, u32[]{:S(2)}, u32[]{:S(2)}) collective-permute-start(f32[72,384]{1,0:T(8,128)S(1)} %fusion.block), channel_id=1, source_target_pairs={{1,2},{3,4},{5,6},{7,8},{9,10},{11,12},{13,14},{15,16},{17,18},{19... | collective-permute-start | bytes 331784 | tf_op jit(solution)/shard_map/ppermute | solution.py:288
